TPU v7x, 32 devices: a whole 2x2x4 slice. The times are simulated.
32 devices in a mesh: seq: 8 (over z, x), img: 2 (over y), fsdp: 2 (over core).
Axes of the slice: x: 2, y: 2, z: 4, core: 2. Of those that a mesh axis runs over, the one named last changes fastest.
Arguments:
- vision_feats: bfloat16 [2, 2304, 1024], P('img', ('seq', 'fsdp')), may hold values from -6 to 6
- ln_gain: float32 [1024], replicated, may hold values from 0.5 to 1.5
- ln_bias: float32 [1024], replicated, may hold values from -3 to 3
- w_in: bfloat16 [1024, 4096], P('fsdp', 'seq'), may hold values from -0.1875 to 0.1875
- b_in: float32 [4096], P('seq'), may hold values from -3 to 3
- w_out: bfloat16 [4096, 4096], P('seq', 'fsdp'), may hold values from -0.09375 to 0.09375
- lm_grad: bfloat16 [2, 4096, 4096], P('img', 'seq', 'fsdp'), may hold values from -0.079589844 to 0.079589844
- image_counts: int32 [2, 2], P('img'), may hold values from 1 to 3, as said below
- token_pos: int32 [2, 2304], P('img'), may hold values from 0 to 2047, as said below
Outputs:
- w_in_grad: float32 [1024, 4096], P(('img', 'fsdp'), 'seq')
- b_in_grad: float32 [4096], replicated
- w_out_grad: float32 [4096, 4096], P(('seq', 'img'), 'fsdp')
- b_out_grad: float32 [4096], replicated
- ln_gain_grad: float32 [1024], replicated
- ln_bias_grad: float32 [1024], replicated
Inputs may be any that keep to these rules, and one draw needn't show every extreme that they name: `image_counts`: in each group the 2 samples hold 4 images together, each sample one or more. `token_pos`: each image's 576 tokens take consecutive positions of its sample's sequence in order; a sample's images come in order without intersection, and images are numbered sample by sample as image_counts gives.
All inputs are finite; a program needn't handle non-finite values.
Results may differ from a plain program's by a relative error of at most 0.0047.
Values may be sent and summed in bfloat16 or wider, within the bound.
A program may use at most 128 MiB of HBM per device.

v0:
```python
import jax
import jax.numpy as jnp
from jax import lax
from jax.sharding import PartitionSpec as P

PATCH = 576
LEN = 2048


def gelu_parts(preact):
    cumul = 0.5 * (1.0 + lax.erf(preact * 0.7071067811865476))
    density = jnp.exp(-0.5 * preact * preact) * 0.3989422804014327
    return (preact * cumul, cumul + preact * density)


def contract(left, right, left_dim, right_dim):
    return lax.dot_general(
        left, right, (((left_dim,), (right_dim,)), ((), ())), preferred_element_type=jnp.float32
    )


def own_columns(matrix, img_count, fsdp_count, fsdp_index):
    rows = matrix.shape[0]
    block = matrix.shape[1] // (img_count * fsdp_count)
    shaped = matrix.reshape(rows, img_count, fsdp_count, block)
    taken = lax.dynamic_index_in_dim(shaped, fsdp_index, axis=2, keepdims=False)
    return taken.reshape(rows, img_count * block)


def place_columns(vector, img_count, fsdp_count, fsdp_index):
    block = vector.shape[0] // img_count
    holder = jnp.zeros((img_count, fsdp_count, block), jnp.float32)
    holder = lax.dynamic_update_slice(
        holder, vector.reshape(img_count, 1, block), (0, fsdp_index, 0)
    )
    return holder.reshape(img_count * fsdp_count * block)


def per_device(vision_feats, ln_gain, ln_bias, w_in, b_in, w_out, lm_grad, image_counts, token_pos):
    seq_count = lax.axis_size("seq")
    seq_index = lax.axis_index("seq")
    img_count = lax.axis_size("img")
    fsdp_count = lax.axis_size("fsdp")
    fsdp_index = lax.axis_index("fsdp")
    lm_block = lm_grad[0]
    block_rows = lm_block.shape[0]
    half_width = lm_block.shape[1]
    position_count = block_rows * seq_count
    counts = image_counts[0]
    positions = token_pos[0]
    row_count = positions.shape[0]
    image_index = jnp.arange(row_count, dtype=jnp.int32) // PATCH
    bounds = jnp.cumsum(counts)
    sample = jnp.sum((image_index[:, None] >= bounds[None, :]).astype(jnp.int32), axis=1)
    abs_pos = sample * LEN + positions
    marker = jnp.zeros((position_count,), jnp.float32).at[abs_pos].set(1.0)
    own_mask = lax.dynamic_slice_in_dim(marker, seq_index * block_rows, block_rows).astype(
        jnp.bfloat16
    )
    out_bias_half = jnp.dot(own_mask[None, :], lm_block, preferred_element_type=jnp.float32)[0]
    out_bias_full = lax.dynamic_update_slice_in_dim(
        jnp.zeros((half_width * fsdp_count,), jnp.float32),
        out_bias_half,
        fsdp_index * half_width,
        0,
    )
    w_in_full = lax.all_gather(w_in, "fsdp", axis=0, tiled=True)
    gathered = lax.all_gather(vision_feats[0], ("seq", "fsdp"), axis=0, tiled=True)
    values = gathered.astype(jnp.float32)
    row_mean = jnp.mean(values, axis=1, keepdims=True)
    centred = values - row_mean
    row_var = jnp.mean(centred * centred, axis=1, keepdims=True)
    normed = centred * lax.rsqrt(row_var + 1e-05)
    normed_in = (normed * ln_gain + ln_bias).astype(jnp.bfloat16)
    preact = jnp.dot(normed_in, w_in_full, preferred_element_type=jnp.float32) + b_in
    activ, slope = gelu_parts(preact)
    hidden = activ.astype(jnp.bfloat16)
    hidden_width = hidden.shape[1]
    whole_grad = lax.all_gather(lm_block, "seq", axis=0, tiled=True)
    picked = whole_grad[abs_pos]
    hidden_part = contract(picked, w_out, 1, 1)
    w_out_part = contract(hidden, picked, 0, 0)
    hidden_grad = lax.psum(hidden_part, "fsdp")
    preact_grad = (hidden_grad * slope).astype(jnp.bfloat16)
    own_normed_in = own_columns(normed_in, img_count, fsdp_count, fsdp_index)
    own_normed = own_columns(normed, img_count, fsdp_count, fsdp_index)
    own_w_in = own_columns(w_in_full.T, img_count, fsdp_count, fsdp_index)
    w_in_part = contract(own_normed_in, preact_grad, 0, 0)
    half_rows = row_count // fsdp_count
    own_rows = lax.dynamic_slice_in_dim(preact_grad, fsdp_index * half_rows, half_rows, 0)
    b_in_part = jnp.sum(own_rows, axis=0, dtype=jnp.float32)
    normed_grad = contract(preact_grad, own_w_in, 1, 0)
    gain_part = place_columns(
        jnp.sum(normed_grad * own_normed, axis=0), img_count, fsdp_count, fsdp_index
    )
    bias_part = place_columns(jnp.sum(normed_grad, axis=0), img_count, fsdp_count, fsdp_index)
    w_in_grad, w_out_grad = (
        lax.psum_scatter(w_in_part, "img", scatter_dimension=0, tiled=True),
        lax.psum_scatter(w_out_part, "img", scatter_dimension=0, tiled=True),
    )
    hidden_full = lax.dynamic_update_slice_in_dim(
        jnp.zeros((hidden_width * seq_count,), jnp.float32), b_in_part, seq_index * hidden_width, 0
    )
    gain_grad, bias_grad, b_in_grad, b_out_grad = lax.psum(
        (gain_part, bias_part, hidden_full, out_bias_full), ("seq", "img", "fsdp")
    )
    return (w_in_grad, b_in_grad, w_out_grad, b_out_grad, gain_grad, bias_grad)


def solution(mesh):
    return jax.shard_map(
        per_device,
        mesh=mesh,
        in_specs=(
            P("img", ("seq", "fsdp"), None),
            P(),
            P(),
            P("fsdp", "seq"),
            P("seq"),
            P("seq", "fsdp"),
            P("img", "seq", "fsdp"),
            P("img", None),
            P("img", None),
        ),
        out_specs=(P(("img", "fsdp"), "seq"), P(), P(("seq", "img"), "fsdp"), P(), P(), P()),
        check_vma=False,
    )
```

profile of v0, /device:TPU:0, one launch (start us, length us, event | category | flops | bytes accessed | tf_op | source)
XLA Modules:
  0.0 437.1 jit_solution(6674310867122269369)
XLA Ops:
  7.2 0.7 all-gather.10.cloned.1.call-update
  8.0 0.7 all-gather.8.cloned.1.call-update
  8.7 0.7 all-gather.6.cloned.1.call-update
  9.5 0.8 reduce-window.8
  10.4 0.7 fusion.17
  11.2 229.0 %all-gather.10.cloned.1.call-done = bf16[1,4096,2048]{2,1,0:T(8,128)(2,1)} async-done(((bf16[1,512,2048]{2,1,0:T(8,128)(2,1)}), bf16[1,4096,2048]{2,1,0:T(8,128)(2,1)}) %all-gather.10.cloned.1.call-update) | async-done | bytes 16777232 | tf_op jit(solution)/shard_map/all_gather | solution.py:79
  240.2 26.3 %gather_fusion = bf16[2304,2048]{1,0:T(8,128)(2,1)} fusion(bf16[4096,2048]{1,0:T(8,128)(2,1)} %bitcast.48, s32[3072]{0:T(1024)S(1)} %pad_clamp_fusion), kind=kCustom, calls=%fused_computation | custom fusion | bytes 18883584 | tf_op jit(solution)/shard_map/gather | solution.py:80
  266.5 11.0 %fusion.21 = f32[2304,512]{1,0:T(8,128)} fusion(bf16[2304,2048]{1,0:T(8,128)(2,1)} %gather_fusion, bf16[512,2048]{1,0:T(8,128)(2,1)S(1)} %copy-done), kind=kOutput, calls=%fused_computation.47 | convolution fusion | flops 4831838208 | bytes 16252928 | tf_op jit(solution)/shard_map/dot_general | solution.py:17
  277.5 0.2 reduce-scatter.3.cloned.1.call-start
  277.8 16.0 %all-gather.8.cloned.1.call-done = bf16[1,2304,1024]{2,1,0:T(8,128)(2,1)} async-done(((bf16[1,144,1024]{2,1,0:T(8,128)(2,1)}), bf16[1,2304,1024]{2,1,0:T(8,128)(2,1)}) %all-gather.8.cloned.1.call-update) | async-done | bytes 4718608 | tf_op jit(solution)/shard_map/all_gather | solution.py:68
  293.8 6.8 %copy.21 = bf16[1,2304,1024]{1,2,0:T(8,128)(2,1)} copy(bf16[1,2304,1024]{2,1,0:T(8,128)(2,1)} %all-gather.8.cloned.1.call-done) | data formatting | bytes 9437184 | tf_op jit(solution)/shard_map/all_gather | solution.py:68
  300.6 3.4 convert_reduce_fusion
  303.9 0.6 copy-done.2
  304.5 1.3 fusion.3
  305.8 4.7 %fusion.1 = (f32[2304,1024]{0,1:T(8,128)}, bf16[2304,1024]{0,1:T(8,128)(2,1)S(1)}) fusion(bf16[1,2304,1024]{1,2,0:T(8,128)(2,1)S(1)} %copy-done.2, f32[2304]{0:T(1024)S(1)} %add_rsqrt_fusion, f32[2304]{0:T(1024)S(1)} %broadcast_multiply_fusion.1, f32[1024]{0:T(1024)S(1)} %copy-done.7, f32[1024]{0:T(1024)S(1)} %copy-done.8), kind=kLoop, calls=%fused_computation.5 | loop fusion | flops 14155776 | bytes 18900992 | tf_op jit(solution)/shard_map/mul | solution.py:73
  310.5 2.3 copy-done.3
  312.8 1.6 constant_dynamic-slice_fusion.2
  314.4 21.0 %all-reduce.3.cloned.1.call-done = f32[2304,512]{1,0:T(8,128)} async-done(((f32[2304,512]{1,0:T(8,128)}), f32[2304,512]{1,0:T(8,128)}) %all-reduce.3.cloned.1.call-update) | async-done | bytes 4718608 | tf_op jit(solution)/shard_map/psum | solution.py:83
  335.4 8.7 %fusion.9 = (bf16[2304,512]{1,0:T(8,128)(2,1)S(1)}, f32[2304,512]{1,0:T(8,128)}) fusion(f32[2304,512]{1,0:T(8,128)} %all-reduce.3.cloned.1.call-done, f32[512]{0:T(512)S(1)} %copy-done.9, bf16[2304,1024]{0,1:T(8,128)(2,1)} %copy-done.3, bf16[1024,512]{1,0:T(8,128)(2,1)} %all-gather.6.cloned.1.call-done), kind=kOutput, calls=%fused_computation.16 | convolution fusion | flops 2428895232 | bytes 17565696 | tf_op jit(solution)/shard_map/dot_general | solution.py:75
  344.1 1.4 copy-done.6
  345.5 2.4 fusion.22
  347.9 11.1 %fusion.10 = f32[512,2048]{1,0:T(8,128)} fusion(bf16[2304,2048]{1,0:T(8,128)(2,1)} %gather_fusion, f32[2304,512]{1,0:T(8,128)} %get-tuple-element.15), kind=kOutput, calls=%fused_computation.20 | convolution fusion | flops 4837736448 | bytes 18350080 | tf_op jit(solution)/shard_map/dot_general | solution.py:17
  359.1 9.2 %scatter_custom_fusion = f32[4096]{0:T(1024)S(1)} fusion(s32[2304]{0:T(1024)S(1)} %fusion.17, f32[2304]{0:T(1024)S(1)} %broadcast.81, f32[]{:T(128)} %constant.21.clone.1), kind=kCustom, calls=%fused_computation.38 | custom fusion | bytes 16388 | tf_op jit(solution)/shard_map/scatter | solution.py:56
  368.4 0.4 fusion.11
  368.8 0.3 dynamic_update_slice.13
  369.1 1.1 constant_dynamic-slice_fusion.1
  370.1 4.9 %constant_dynamic-slice_fusion = f32[2304,2,1,256]{0,3,2,1:T(8,128)} fusion(f32[2304,2,2,256]{0,3,2,1:T(8,128)} %bitcast.49, s32[]{:T(128)S(6)} %select_n.40), kind=kLoop, calls=%fused_computation.43 | loop fusion | bytes 9437188 | tf_op jit(solution)/shard_map/jit(dynamic_index_in_dim)/dynamic_slice | solution.py:26
  375.0 6.1 %copy.24 = f32[2304,512]{1,0:T(8,128)} copy(f32[2304,512]{0,1:T(8,128)} %bitcast.50) | data formatting | bytes 9437184 | tf_op jit(solution)/shard_map/reshape | solution.py:27
  381.2 4.6 %fusion.20 = (f32[512]{0:T(512)S(1)}, f32[512]{0:T(512)S(1)}) fusion(f32[2304,512]{1,0:T(8,128)} %copy.24, bf16[2304,512]{1,0:T(8,128)(2,1)} %copy-done.6, bf16[512,512]{0,1:T(8,128)(2,1)S(1)} %bitcast.53), kind=kOutput, calls=%fused_computation.46 | convolution fusion | flops 1211497472 | bytes 7606272 | tf_op jit(solution)/shard_map/dot_general | solution.py:17
  385.9 1.5 convert_reduce_fusion.1
  387.4 0.3 dynamic_update_slice.12
  387.7 42.6 %all-reduce = (f32[4096]{0:T(1024)}, f32[4096]{0:T(1024)}, f32[1024]{0:T(1024)}, f32[1024]{0:T(1024)}) all-reduce(f32[4096]{0:T(1024)S(1)} %dynamic_update_slice.12, f32[4096]{0:T(1024)S(1)} %dynamic_update_slice.13, f32[1024]{0:T(1024)S(1)} %bitcast.57, ...), channel_id=1, replica_groups=mesh['seq'=8,'img'=2,'fsdp'=2] {'seq','img','fsdp'}, use_global_device_ids=true, to_apply=%region_7.8 | all-reduce | flops 10240 | bytes 81920 | tf_op jit(solution)/shard_map/psum | solution.py:104
  (45 shorter events, 0.6 us)
Async XLA Ops:
  7.2 259.3 %copy-start = (bf16[512,2048]{1,0:T(8,128)(2,1)S(1)}, bf16[512,2048]{1,0:T(8,128)(2,1)}, u32[]{:S(2)}) copy-start(bf16[512,2048]{1,0:T(8,128)(2,1)} %param.14) | copy-start | bytes 6291460
  7.2 233.0 %all-gather.10.cloned.1.call-start = ((), (), s32[]{:S(2)}) async-start(), calls=%async_computation.7 | async-start | bytes 18874368 | tf_op jit(solution)/shard_map/all_gather | solution.py:79
  7.9 285.9 %all-gather.8.cloned.1.call-start = ((), (), s32[]{:S(2)}) async-start(), calls=%async_computation.6 | async-start | bytes 5013504 | tf_op jit(solution)/shard_map/all_gather | solution.py:68
  8.7 305.7 %all-gather.6.cloned.1.call-start = ((), (), s32[]{:S(2)}) async-start(), calls=%async_computation.3 | async-start | bytes 1572864 | tf_op jit(solution)/shard_map/all_gather | solution.py:67
  9.4 326.0 %all-reduce.3.cloned.1.call-start = ((), (), s32[]{:S(2)}) async-start(), calls=%async_computation.2 | async-start | bytes 9437184 | tf_op jit(solution)/shard_map/psum | solution.py:83
  277.5 152.7 %reduce-scatter.3.cloned.1.call-start = ((), (), s32[]{:S(2)}) async-start(), calls=%async_computation.4 | async-start | bytes 1572864 | tf_op jit(solution)/shard_map/reduce_scatter | solution.py:98
  300.6 4.0 copy-start.2
  300.6 5.3 %copy-start.7 = (f32[1024]{0:T(1024)S(1)}, f32[1024]{0:T(1024)}, u32[]{:S(2)}) copy-start(f32[1024]{0:T(1024)} %param.11) | copy-start | bytes 12292
  300.6 5.3 %copy-start.8 = (f32[1024]{0:T(1024)S(1)}, f32[1024]{0:T(1024)}, u32[]{:S(2)}) copy-start(f32[1024]{0:T(1024)} %param.10) | copy-start | bytes 12292
  310.5 2.3 copy-start.3
  310.5 24.8 %copy-start.9 = (f32[512]{0:T(512)S(1)}, f32[512]{0:T(512)}, u32[]{:S(2)}) copy-start(f32[512]{0:T(512)} %param.13) | copy-start | bytes 6148
  335.4 10.1 %copy-start.5 = (bf16[2304,2,1,256]{0,3,2,1:T(8,128)(2,1)S(1)}, bf16[2304,2,1,256]{0,3,2,1:T(8,128)(2,1)}, u32[]{:S(2)}) copy-start(bf16[2304,2,1,256]{0,3,2,1:T(8,128)(2,1)} %constant_dynamic-slice_fusion.2) | copy-start | bytes 7077892
  344.1 1.4 copy-start.6
  347.9 82.4 %reduce-scatter.5.cloned.1.call-start = ((), (), s32[]{:S(2)}) async-start(), calls=%async_computation.5 | async-start | bytes 6291456 | tf_op jit(solution)/shard_map/reduce_scatter | solution.py:99
  347.9 20.5 %copy-start.4 = (bf16[1,512,2048]{2,1,0:T(8,128)(2,1)S(1)}, bf16[1,512,2048]{2,1,0:T(8,128)(2,1)}, u32[]{:S(2)}) copy-start(bf16[1,512,2048]{2,1,0:T(8,128)(2,1)} %param.15) | copy-start | bytes 6291460
  381.2 49.1 %copy-start.1 = (bf16[512,2048]{1,0:T(8,128)(2,1)S(1)}, bf16[512,2048]{1,0:T(8,128)(2,1)}, u32[]{:S(2)}) copy-start(bf16[512,2048]{1,0:T(8,128)(2,1)} %param.14) | copy-start | bytes 6291460
Sparse Core Ops, SparseCore 0:
  10.1 229.9 all-gather.9
  242.4 51.2 all-gather.7
  295.3 7.5 all-gather.5
  305.3 30.0 all-reduce.2
  348.0 21.5 reduce-scatter.2
  372.3 55.2 reduce-scatter.4
where the time goes:
time: 438 us; the launch traced here: 437 us
  waiting for transfers between devices  268 us (61%)
  local copies, waits for them, and re-layouts  61 us (14%)
  blocking collectives  42.6 us (10%)
  matrix products  38.2 us (9%)
  between operations  14.2 us (3%)
  other arithmetic  12.6 us (3%)
    all_gather x1, waiting for transfers between devices, per_device(): whole_grad = lax.all_gather(lm_block, 'seq', axis=0, tiled=True)  229 us
    psum x1, blocking collectives, per_device(): lax.psum((gain_part, bias_part, hidden_full, out_bias_full), ('seq', 'img...  42.6 us
    dot_general x4, matrix products, contract(): lax.dot_general(left, right, (((left_dim,), (right_dim,)), ((), ())), pre...  29.2 us
    gather x1, local copies, waits for them, and re-layouts, per_device(): picked = whole_grad[abs_pos]  26.3 us
    psum x1, waiting for transfers between devices, per_device(): hidden_grad = lax.psum(hidden_part, 'fsdp')  21 us
    all_gather x1, waiting for transfers between devices, per_device(): lax.all_gather(vision_feats[0], ('seq', 'fsdp'), axis=0, tiled=True)  16 us
    scatter x1, local copies, waits for them, and re-layouts, per_device(): marker = jnp.zeros((position_count,), jnp.float32).at[abs_pos].set(1.0)  9.21 us
  transfers between devices with their start and end apart: 6, of which 3 were waited for; matrix products, arithmetic and copies ran while one was open for 22% of the time, Pallas kernels for 0%

commit v1 on v0

--- a/solution.py
+++ b/solution.py
@@ -102,7 +102,7 @@
         jnp.zeros((hidden_width * seq_count,), jnp.float32), b_in_part, seq_index * hidden_width, 0
     )
     gain_grad, bias_grad, b_in_grad, b_out_grad = lax.psum(
-        (gain_part, bias_part, hidden_full, out_bias_full), ("seq", "img", "fsdp")
+        lax.psum((gain_part, bias_part, hidden_full, out_bias_full), ("img", "fsdp")), "seq"
     )
     return (w_in_grad, b_in_grad, w_out_grad, b_out_grad, gain_grad, bias_grad)
 

time: 438 us -> 447 us (1.021)
  blocking collectives: 42.6 us -> 52.3 us
    psum x1 -> x2, blocking collectives: 42.6 us -> 52.3 us  [the longest x1 38.1 us: per_device(): lax.psum(lax.psum((gain_part, bias_part, hidden_full, out_bias_full), ('i...]
where the time goes in v1:
time: 447 us
  waiting for transfers between devices  268 us (60%)
  local copies, waits for them, and re-layouts  61 us (14%)
  blocking collectives  52.3 us (12%)
  matrix products  38.2 us (9%)
  between operations  14.2 us (3%)
  other arithmetic  12.6 us (3%)
    all_gather x1, waiting for transfers between devices, per_device(): whole_grad = lax.all_gather(lm_block, 'seq', axis=0, tiled=True)  229 us
    psum x1, blocking collectives, per_device(): lax.psum(lax.psum((gain_part, bias_part, hidden_full, out_bias_full), ('i...  38.1 us
    dot_general x4, matrix products, contract(): lax.dot_general(left, right, (((left_dim,), (right_dim,)), ((), ())), pre...  29.2 us
    gather x1, local copies, waits for them, and re-layouts, per_device(): picked = whole_grad[abs_pos]  26.3 us
    psum x1, waiting for transfers between devices, per_device(): hidden_grad = lax.psum(hidden_part, 'fsdp')  21 us
    all_gather x1, waiting for transfers between devices, per_device(): lax.all_gather(vision_feats[0], ('seq', 'fsdp'), axis=0, tiled=True)  16 us
    psum x1, blocking collectives, per_device(): lax.psum((gain_part, bias_part, hidden_full, out_bias_full), ('img', 'fsd...  14.2 us
    scatter x1, local copies, waits for them, and re-layouts, per_device(): marker = jnp.zeros((position_count,), jnp.float32).at[abs_pos].set(1.0)  9.21 us
  transfers between devices with their start and end apart: 6, of which 3 were waited for; matrix products, arithmetic and copies ran while one was open for 22% of the time, Pallas kernels for 0%

profile of v1, /device:TPU:0, one launch (start us, length us, event | category | flops | bytes accessed | tf_op | source)
XLA Modules:
  0.0 446.9 jit_solution(11221132149485244769)
XLA Ops:
  7.2 0.7 all-gather.10.cloned.1.call-update
  8.0 0.7 all-gather.8.cloned.1.call-update
  8.7 0.7 all-gather.6.cloned.1.call-update
  9.5 0.8 reduce-window.8
  10.4 0.7 fusion.17
  11.2 229.0 %all-gather.10.cloned.1.call-done = bf16[1,4096,2048]{2,1,0:T(8,128)(2,1)} async-done(((bf16[1,512,2048]{2,1,0:T(8,128)(2,1)}), bf16[1,4096,2048]{2,1,0:T(8,128)(2,1)}) %all-gather.10.cloned.1.call-update) | async-done | bytes 16777232 | tf_op jit(solution)/shard_map/all_gather | solution.py:79
  240.2 26.3 %gather_fusion = bf16[2304,2048]{1,0:T(8,128)(2,1)} fusion(bf16[4096,2048]{1,0:T(8,128)(2,1)} %bitcast.48, s32[3072]{0:T(1024)S(1)} %pad_clamp_fusion), kind=kCustom, calls=%fused_computation | custom fusion | bytes 18883584 | tf_op jit(solution)/shard_map/gather | solution.py:80
  266.5 11.0 %fusion.21 = f32[2304,512]{1,0:T(8,128)} fusion(bf16[2304,2048]{1,0:T(8,128)(2,1)} %gather_fusion, bf16[512,2048]{1,0:T(8,128)(2,1)S(1)} %copy-done), kind=kOutput, calls=%fused_computation.47 | convolution fusion | flops 4831838208 | bytes 16252928 | tf_op jit(solution)/shard_map/dot_general | solution.py:17
  277.8 16.0 %all-gather.8.cloned.1.call-done = bf16[1,2304,1024]{2,1,0:T(8,128)(2,1)} async-done(((bf16[1,144,1024]{2,1,0:T(8,128)(2,1)}), bf16[1,2304,1024]{2,1,0:T(8,128)(2,1)}) %all-gather.8.cloned.1.call-update) | async-done | bytes 4718608 | tf_op jit(solution)/shard_map/all_gather | solution.py:68
  293.8 6.8 %copy.21 = bf16[1,2304,1024]{1,2,0:T(8,128)(2,1)} copy(bf16[1,2304,1024]{2,1,0:T(8,128)(2,1)} %all-gather.8.cloned.1.call-done) | data formatting | bytes 9437184 | tf_op jit(solution)/shard_map/all_gather | solution.py:68
  300.6 3.4 convert_reduce_fusion
  303.9 0.6 copy-done.2
  304.5 1.3 fusion.3
  305.8 4.7 %fusion.1 = (f32[2304,1024]{0,1:T(8,128)}, bf16[2304,1024]{0,1:T(8,128)(2,1)S(1)}) fusion(bf16[1,2304,1024]{1,2,0:T(8,128)(2,1)S(1)} %copy-done.2, f32[2304]{0:T(1024)S(1)} %add_rsqrt_fusion, f32[2304]{0:T(1024)S(1)} %broadcast_multiply_fusion.1, f32[1024]{0:T(1024)S(1)} %copy-done.7, f32[1024]{0:T(1024)S(1)} %copy-done.8), kind=kLoop, calls=%fused_computation.5 | loop fusion | flops 14155776 | bytes 18900992 | tf_op jit(solution)/shard_map/mul | solution.py:73
  310.5 2.3 copy-done.3
  312.8 1.6 constant_dynamic-slice_fusion.2
  314.4 21.0 %all-reduce.4.cloned.1.call-done = f32[2304,512]{1,0:T(8,128)} async-done(((f32[2304,512]{1,0:T(8,128)}), f32[2304,512]{1,0:T(8,128)}) %all-reduce.4.cloned.1.call-update) | async-done | bytes 4718608 | tf_op jit(solution)/shard_map/psum | solution.py:83
  335.4 8.7 %fusion.9 = (bf16[2304,512]{1,0:T(8,128)(2,1)S(1)}, f32[2304,512]{1,0:T(8,128)}) fusion(f32[2304,512]{1,0:T(8,128)} %all-reduce.4.cloned.1.call-done, f32[512]{0:T(512)S(1)} %copy-done.9, bf16[2304,1024]{0,1:T(8,128)(2,1)} %copy-done.3, bf16[1024,512]{1,0:T(8,128)(2,1)} %all-gather.6.cloned.1.call-done), kind=kOutput, calls=%fused_computation.16 | convolution fusion | flops 2428895232 | bytes 17565696 | tf_op jit(solution)/shard_map/dot_general | solution.py:75
  344.1 1.4 copy-done.6
  345.5 2.4 fusion.22
  347.9 11.1 %fusion.10 = f32[512,2048]{1,0:T(8,128)} fusion(bf16[2304,2048]{1,0:T(8,128)(2,1)} %gather_fusion, f32[2304,512]{1,0:T(8,128)} %get-tuple-element.19), kind=kOutput, calls=%fused_computation.20 | convolution fusion | flops 4837736448 | bytes 18350080 | tf_op jit(solution)/shard_map/dot_general | solution.py:17
  359.1 9.2 %scatter_custom_fusion = f32[4096]{0:T(1024)S(1)} fusion(s32[2304]{0:T(1024)S(1)} %fusion.17, f32[2304]{0:T(1024)S(1)} %broadcast.81, f32[]{:T(128)} %constant.21.clone.1), kind=kCustom, calls=%fused_computation.38 | custom fusion | bytes 16388 | tf_op jit(solution)/shard_map/scatter | solution.py:56
  368.4 0.4 fusion.11
  368.8 0.3 dynamic_update_slice.13
  369.1 1.1 constant_dynamic-slice_fusion.1
  370.1 4.9 %constant_dynamic-slice_fusion = f32[2304,2,1,256]{0,3,2,1:T(8,128)} fusion(f32[2304,2,2,256]{0,3,2,1:T(8,128)} %bitcast.49, s32[]{:T(128)S(6)} %select_n.40), kind=kLoop, calls=%fused_computation.43 | loop fusion | bytes 9437188 | tf_op jit(solution)/shard_map/jit(dynamic_index_in_dim)/dynamic_slice | solution.py:26
  375.0 6.1 %copy.24 = f32[2304,512]{1,0:T(8,128)} copy(f32[2304,512]{0,1:T(8,128)} %bitcast.50) | data formatting | bytes 9437184 | tf_op jit(solution)/shard_map/reshape | solution.py:27
  381.2 4.6 %fusion.20 = (f32[512]{0:T(512)S(1)}, f32[512]{0:T(512)S(1)}) fusion(f32[2304,512]{1,0:T(8,128)} %copy.24, bf16[2304,512]{1,0:T(8,128)(2,1)} %copy-done.6, bf16[512,512]{0,1:T(8,128)(2,1)S(1)} %bitcast.53), kind=kOutput, calls=%fused_computation.46 | convolution fusion | flops 1211497472 | bytes 7606272 | tf_op jit(solution)/shard_map/dot_general | solution.py:17
  385.9 1.5 convert_reduce_fusion.1
  387.4 0.3 dynamic_update_slice.12
  387.7 14.2 %all-reduce.1 = (f32[4096]{0:T(1024)S(1)}, f32[4096]{0:T(1024)S(1)}, f32[1024]{0:T(1024)S(1)}, f32[1024]{0:T(1024)S(1)}) all-reduce(f32[4096]{0:T(1024)S(1)} %dynamic_update_slice.12, f32[4096]{0:T(1024)S(1)} %dynamic_update_slice.13, f32[1024]{0:T(1024)S(1)} %bitcast.57, ...), channel_id=1, replica_groups=mesh['seq'=8,'img'=2,'fsdp'=2] {'img','fsdp'}, use_global_device_ids=true, to_apply=%region_7.8 | all-reduce | flops 10240 | bytes 81920 | tf_op jit(solution)/shard_map/psum | solution.py:105
  401.9 38.1 %all-reduce = (f32[4096]{0:T(1024)}, f32[4096]{0:T(1024)}, f32[1024]{0:T(1024)}, f32[1024]{0:T(1024)}) all-reduce(f32[4096]{0:T(1024)S(1)} %get-tuple-element.12, f32[4096]{0:T(1024)S(1)} %get-tuple-element.13, f32[1024]{0:T(1024)S(1)} %get-tuple-element.14, ...), channel_id=1, replica_groups=mesh['seq'=8,'img'=2,'fsdp'=2] {'seq'}, use_global_device_ids=true, to_apply=%region_8.9 | all-reduce | flops 10240 | bytes 81920 | tf_op jit(solution)/shard_map/psum | solution.py:104
  (46 shorter events, 0.9 us)
Async XLA Ops:
  7.2 259.3 %copy-start = (bf16[512,2048]{1,0:T(8,128)(2,1)S(1)}, bf16[512,2048]{1,0:T(8,128)(2,1)}, u32[]{:S(2)}) copy-start(bf16[512,2048]{1,0:T(8,128)(2,1)} %param.14) | copy-start | bytes 6291460
  7.2 233.0 %all-gather.10.cloned.1.call-start = ((), (), s32[]{:S(2)}) async-start(), calls=%async_computation.7 | async-start | bytes 18874368 | tf_op jit(solution)/shard_map/all_gather | solution.py:79
  7.9 285.9 %all-gather.8.cloned.1.call-start = ((), (), s32[]{:S(2)}) async-start(), calls=%async_computation.6 | async-start | bytes 5013504 | tf_op jit(solution)/shard_map/all_gather | solution.py:68
  8.7 305.7 %all-gather.6.cloned.1.call-start = ((), (), s32[]{:S(2)}) async-start(), calls=%async_computation.3 | async-start | bytes 1572864 | tf_op jit(solution)/shard_map/all_gather | solution.py:67
  9.4 326.0 %all-reduce.4.cloned.1.call-start = ((), (), s32[]{:S(2)}) async-start(), calls=%async_computation.2 | async-start | bytes 9437184 | tf_op jit(solution)/shard_map/psum | solution.py:83
  277.5 162.5 %reduce-scatter.3.cloned.1.call-start = ((), (), s32[]{:S(2)}) async-start(), calls=%async_computation.4 | async-start | bytes 1572864 | tf_op jit(solution)/shard_map/reduce_scatter | solution.py:98
  300.6 4.0 copy-start.2
  300.6 5.3 %copy-start.7 = (f32[1024]{0:T(1024)S(1)}, f32[1024]{0:T(1024)}, u32[]{:S(2)}) copy-start(f32[1024]{0:T(1024)} %param.11) | copy-start | bytes 12292
  300.6 5.3 %copy-start.8 = (f32[1024]{0:T(1024)S(1)}, f32[1024]{0:T(1024)}, u32[]{:S(2)}) copy-start(f32[1024]{0:T(1024)} %param.10) | copy-start | bytes 12292
  310.5 2.3 copy-start.3
  310.5 24.8 %copy-start.9 = (f32[512]{0:T(512)S(1)}, f32[512]{0:T(512)}, u32[]{:S(2)}) copy-start(f32[512]{0:T(512)} %param.13) | copy-start | bytes 6148
  335.4 10.1 %copy-start.5 = (bf16[2304,2,1,256]{0,3,2,1:T(8,128)(2,1)S(1)}, bf16[2304,2,1,256]{0,3,2,1:T(8,128)(2,1)}, u32[]{:S(2)}) copy-start(bf16[2304,2,1,256]{0,3,2,1:T(8,128)(2,1)} %constant_dynamic-slice_fusion.2) | copy-start | bytes 7077892
  344.1 1.4 copy-start.6
  347.9 92.2 %reduce-scatter.5.cloned.1.call-start = ((), (), s32[]{:S(2)}) async-start(), calls=%async_computation.5 | async-start | bytes 6291456 | tf_op jit(solution)/shard_map/reduce_scatter | solution.py:99
  347.9 20.5 %copy-start.4 = (bf16[1,512,2048]{2,1,0:T(8,128)(2,1)S(1)}, bf16[1,512,2048]{2,1,0:T(8,128)(2,1)}, u32[]{:S(2)}) copy-start(bf16[1,512,2048]{2,1,0:T(8,128)(2,1)} %param.15) | copy-start | bytes 6291460
  381.2 58.9 %copy-start.1 = (bf16[512,2048]{1,0:T(8,128)(2,1)S(1)}, bf16[512,2048]{1,0:T(8,128)(2,1)}, u32[]{:S(2)}) copy-start(bf16[512,2048]{1,0:T(8,128)(2,1)} %param.14) | copy-start | bytes 6291460
Sparse Core Ops, SparseCore 0:
  10.1 229.9 all-gather.9
  242.4 51.2 all-gather.7
  295.3 7.5 all-gather.5
  305.3 30.0 all-reduce.3
  348.0 21.5 reduce-scatter.2
  372.3 55.1 reduce-scatter.4
